TPU v7x, 32 devices: a whole 2x2x4 slice. The times are simulated.
32 devices in a mesh: gx: 4 (over y, core), gy: 8 (over z, x).
Axes of the slice: x: 2, y: 2, z: 4, core: 2. Of those that a mesh axis runs over, the one named last changes fastest.
Arguments:
- position: float32 [4, 8, 3, 4096], P('gx', 'gy'), may hold values from 0 to 8, as said below
- velocity: float32 [4, 8, 3, 4096], P('gx', 'gy'), may hold values from -6 to 6
- mass: float32 [4, 8, 1, 4096], P('gx', 'gy'), may hold values from 0.3 to 3
- pair_list: int32 [4, 8, 32, 27], P('gx', 'gy'), may hold values from 0 to 287, as said below
- hot_leaf: int32 [4, 8, 8], P('gx', 'gy'), may hold values from 0 to 32, as said below
Outputs:
- displacement: float32 [4, 8, 3, 4096], P('gx', 'gy')
- new_velocity: float32 [4, 8, 3, 4096], P('gx', 'gy')
Inputs may be any that keep to these rules, and one draw needn't show every extreme that they name: `pair_list`: entry k of every list names a leaf of neighbourhood block k mod 9. `position`: component 0 of a particle of cell (i, j) lies in [i, i + 1), component 1 in [j, j + 1), component 2 in [0, 1). `hot_leaf`: the slots of a cell hold distinct leaf numbers first and the empty mark 32 after them; cell (i, j) and cell (i, (j + 4) mod 8) hold exactly 8 hot leaves together.
All inputs are finite; a program needn't handle non-finite values.
Results may differ from a plain program's by a relative error of at most 0.00023.
Values sent between devices are 32-bit elements; how exact they have to be, the bound alone decides.
A program may use at most 64 MiB of HBM per device.

v0:
```python
import functools

import jax
import jax.numpy as jnp
from jax import lax
from jax.experimental import pallas as pl
from jax.experimental.pallas import tpu as pltpu
from jax.sharding import PartitionSpec as P

LEAF = 128
MESH = pl.DeviceIdType.MESH

kernel_scale = 1.0
viscosity = 0.5
time_step = 0.5
base_entries = 9
COORD = (2.0 * 1.4426950408889634 / kernel_scale) ** 0.5


def exchange(sizes, own_ref, out_ref, send_sem, recv_sem):
    count_x, count_y = sizes
    gx, gy = lax.axis_index("gx"), lax.axis_index("gy")

    def inside(a, b):
        terms = []
        if a != 1:
            terms.append(gx > 0 if a == 0 else gx < count_x - 1)
        if b != 1:
            terms.append(gy > 0 if b == 0 else gy < count_y - 1)
        return terms[0] if len(terms) == 1 else terms[0] & terms[1]

    def device(a, b):
        return (jnp.clip(gx + a - 1, 0, count_x - 1), jnp.clip(gy + b - 1, 0, count_y - 1))

    sides = ((1, 0), (1, 2), (0, 1), (2, 1))
    barrier = pltpu.get_barrier_semaphore()
    for a, b in sides:

        @pl.when(inside(a, b))
        def _():
            pl.semaphore_signal(barrier, inc=1, device_id=device(a, b), device_id_type=MESH)

    pl.semaphore_wait(barrier, sum(inside(a, b).astype(jnp.int32) for a, b in sides))

    def copy(source, block, to):
        return pltpu.make_async_remote_copy(
            src_ref=source,
            dst_ref=out_ref.at[block],
            send_sem=send_sem.at[block],
            recv_sem=recv_sem.at[block],
            device_id=device(*to),
            device_id_type=MESH,
        )

    def sent(a, b):
        to = (1, 2 - b) if a == 1 else (2 - a, 1)
        source = own_ref if a == 1 or b == 1 else out_ref.at[3 + b]
        return copy(source, 3 * a + b, to), inside(*to) if a == 1 or b == 1 else inside(2 - a, b)

    for a, b in sides:
        descriptor, valid = sent(a, b)
        pl.when(valid)(descriptor.start)
    out_ref[4] = own_ref[...]
    for a in range(3):
        for b in range(3):
            if (a, b) != (1, 1):

                @pl.when(jnp.logical_not(inside(a, b)))
                def _():
                    out_ref[3 * a + b] = jnp.zeros(own_ref.shape, own_ref.dtype)

    for b in (0, 2):
        pl.when(inside(1, b))(sent(1, b)[0].wait_recv)
        for a in (0, 2):
            descriptor, valid = sent(a, b)
            pl.when(valid)(descriptor.start)
    for a, b in ((0, 1), (2, 1), (0, 0), (2, 0), (0, 2), (2, 2)):
        pl.when(inside(a, b))(sent(a, b)[0].wait_recv)
    for a in range(3):
        for b in range(3):
            if (a, b) != (1, 1):
                descriptor, valid = sent(a, b)
                pl.when(valid)(descriptor.wait_send)


def surround(cell, number):
    channels, width = cell.shape
    count = width // LEAF
    vmem = pl.BlockSpec(memory_space=pltpu.VMEM)
    out = pl.pallas_call(
        functools.partial(exchange, (lax.axis_size("gx"), lax.axis_size("gy"))),
        out_shape=jax.ShapeDtypeStruct((9, channels * count, LEAF), cell.dtype),
        in_specs=[vmem],
        out_specs=vmem,
        scratch_shapes=[pltpu.SemaphoreType.DMA((9,)), pltpu.SemaphoreType.DMA((9,))],
        compiler_params=pltpu.CompilerParams(collective_id=number, has_side_effects=True),
    )(cell.reshape(channels * count, LEAF))
    return out.reshape(9, channels, width)


def split3(value):
    first = value.astype(jnp.bfloat16).astype(jnp.float32)
    rest = value - first
    second = rest.astype(jnp.bfloat16).astype(jnp.float32)
    third = (rest - second).astype(jnp.bfloat16).astype(jnp.float32)
    return first, second, third


def coordinate_rows(x, ones_first):
    a = COORD * x
    c = -0.5 * jnp.sum(a * a, axis=0, keepdims=True)
    one = jnp.ones_like(c)
    pad = jnp.zeros_like(a)
    return jnp.concatenate([a, one, c, pad] if ones_first else [a, c, one, pad], axis=0)


def pair_sums(sections, counts, src_ref, leaf_ref, live_ref, *refs):
    place_refs, channel_refs = refs[:sections], refs[sections : 2 * sections]
    out_refs = refs[2 * sections : 3 * sections]
    feature, target, channel = refs[3 * sections :]
    base_items, entries = counts
    blocks, _, width = place_refs[0].shape
    step = min(width, 8 * LEAF)
    own = blocks // 2
    for place_ref, channel_ref, out_ref in zip(place_refs, channel_refs, out_refs):
        for block in range(blocks):

            def prepare(i, carry):
                span = pl.ds(pl.multiple_of(i * step, step), step)
                rows = coordinate_rows(place_ref[block, 0:3, span], True)
                s1, s2, s3 = split3(rows)
                feature[block, :, span] = jnp.concatenate(
                    [s1, s2, s1, s2, s3, s1], axis=0
                ).astype(jnp.bfloat16)
                c1, c2, _ = split3(channel_ref[block, :, span])
                channel[block, :, span] = jnp.concatenate([c1, c2], axis=0).astype(jnp.bfloat16)
                return carry

            lax.fori_loop(0, width // step, prepare, 0)

        def prepare_target(i, carry):
            span = pl.ds(pl.multiple_of(i * LEAF, LEAF), LEAF)
            rows = coordinate_rows(place_ref[own, 0:3, span], False)
            t1, t2, t3 = split3(rows)
            stack = jnp.concatenate(
                [t1, t1, t2, t2, t1, t3, jnp.zeros((LEAF - 48, LEAF), jnp.float32)], axis=0
            )
            target[i] = stack.T.astype(jnp.bfloat16)
            return carry

        lax.fori_loop(0, width // LEAF, prepare_target, 0)

        def sums(item):
            leaf = leaf_ref[item]
            spans = [
                pl.ds(pl.multiple_of(src_ref[item * entries + k] * LEAF, LEAF), LEAF)
                for k in range(entries)
            ]
            near = jnp.concatenate([feature[k, :, spans[k]] for k in range(entries)], axis=1)
            exponent = jnp.dot(
                target[leaf][:, 0:48], near, preferred_element_type=jnp.float32
            )
            weight = jnp.exp2(exponent).astype(jnp.bfloat16)
            rows = jnp.concatenate([channel[k, :, spans[k]] for k in range(entries)], axis=1)
            both = lax.dot_general(
                rows, weight, (((1,), (1,)), ((), ())), preferred_element_type=jnp.float32
            )
            return leaf, both[0:8] + both[8:16]

        def base(i, carry):
            for u in range(4):
                leaf, value = sums(i * 4 + u)
                out_ref[leaf] = value
            return carry

        lax.fori_loop(0, base_items // 4, base, 0)

        def extra(i, carry):
            leaf, first = sums(base_items + 2 * i)
            _, second = sums(base_items + 2 * i + 1)
            out_ref[leaf] = out_ref[leaf] + (first + second)
            return carry

        lax.fori_loop(0, live_ref[0], extra, 0)


def all_sums(tables, places, channels):
    src, leaves, live, base_items = tables
    sections = len(places)
    blocks, _, width = places[0].shape
    count = width // LEAF
    smem = pl.BlockSpec(memory_space=pltpu.SMEM)
    vmem = pl.BlockSpec(memory_space=pltpu.VMEM)
    outs = pl.pallas_call(
        functools.partial(pair_sums, sections, (base_items, base_entries)),
        out_shape=[jax.ShapeDtypeStruct((count, 8, LEAF), jnp.float32)] * sections,
        in_specs=[smem] * 3 + [vmem] * (2 * sections),
        out_specs=[vmem] * sections,
        scratch_shapes=[
            pltpu.VMEM((blocks, 48, width), jnp.bfloat16),
            pltpu.VMEM((count, LEAF, LEAF), jnp.bfloat16),
            pltpu.VMEM((blocks, 16, width), jnp.bfloat16),
        ],
    )(src, leaves, live, *places, *channels)
    return [jnp.transpose(out, (1, 0, 2)).reshape(8, width) for out in outs]


def local(position, velocity, mass, pair_list, hot_leaf):
    pairs = pair_list[0, 0]
    hot = hot_leaf[0, 0]
    leaf_count, listed = pairs.shape
    groups = listed // base_entries
    lists = (pairs % leaf_count).reshape(leaf_count, groups, base_entries)
    alive = hot < leaf_count
    slot_leaf = jnp.minimum(hot, leaf_count - 1)
    extra_src = jnp.take(lists, slot_leaf, axis=0)[:, 1:]
    src = jnp.concatenate([lists[:, 0].reshape(-1), extra_src.reshape(-1)])
    leaves = jnp.concatenate(
        [jnp.arange(leaf_count, dtype=jnp.int32), jnp.repeat(slot_leaf, groups - 1)]
    )
    live = jnp.sum(alive.astype(jnp.int32)).reshape(1)
    tables = (src, leaves, live, leaf_count)

    centre = jnp.stack(
        [
            lax.axis_index("gx").astype(jnp.float32) + 0.5,
            lax.axis_index("gy").astype(jnp.float32) + 0.5,
            jnp.float32(0.5),
        ]
    ).reshape(1, 3, 1)
    own = base_entries // 2
    state = surround(jnp.concatenate([position, velocity, mass], axis=2)[0, 0], 0)
    pos, vel, m = state[:, 0:3], state[:, 3:6], state[:, 6:7]
    x1 = pos - centre
    x2 = (pos + 0.5 * time_step * vel) - centre
    zeros7 = jnp.zeros((m.shape[0], 7, m.shape[2]), jnp.float32)
    mass_rows = jnp.concatenate([m, zeros7], axis=1)
    rho1, rho2 = all_sums(tables, [x1, x2], [mass_rows, mass_rows])
    own_m = mass[0, 0]
    q_own = 1.0 / (own_m + jnp.concatenate([rho1[0:1], rho2[0:1]], axis=0))
    q_all = surround(q_own, 1)

    def acceleration(x, v, own_v, q, own_q):
        mq = m * q
        rows = jnp.concatenate([m, m * x, mq, mq * (viscosity * v - (2.0 / kernel_scale) * x)], axis=1)
        (s,) = all_sums(tables, [x], [rows])
        own_x = x[own]
        pushed = (2.0 / kernel_scale) * (
            own_q * (own_x * s[0:1] - s[1:4]) + own_x * s[4:5]
        )
        return pushed - viscosity * own_v * s[4:5] + s[5:8]

    own_v = velocity[0, 0]
    acc1 = acceleration(x1, vel, own_v, q_all[:, 0:1], q_own[0:1])
    mid_velocity = own_v + 0.5 * time_step * acc1
    mid_all = surround(mid_velocity, 2)
    acc2 = acceleration(x2, mid_all, mid_velocity, q_all[:, 1:2], q_own[1:2])
    return (
        (time_step * mid_velocity)[None, None],
        (own_v + time_step * acc2)[None, None],
    )


def solution(mesh):
    return jax.shard_map(
        local,
        mesh=mesh,
        in_specs=(
            P("gx", "gy", None, None),
            P("gx", "gy", None, None),
            P("gx", "gy", None, None),
            P("gx", "gy", None, None),
            P("gx", "gy", None),
        ),
        out_specs=(P("gx", "gy", None, None), P("gx", "gy", None, None)),
        check_vma=False,
    )
```

profile of v0, /device:TPU:17, one launch (start us, length us, event | category | flops | bytes accessed | tf_op | source)
XLA Modules:
  0.0 133.4 jit_solution(3161044642790751734)
XLA Ops:
  0.6 1.6 %pad_maximum_fusion.2 = f32[1,1,7,4096]{3,1,2,0:T(1,128)} fusion(f32[1,1,1,4096]{3,1,2,0:T(1,128)} %bitcast.142, f32[1,1,3,4096]{3,1,2,0:T(1,128)} %param.6, f32[1,1,3,4096]{3,1,2,0:T(1,128)} %param.5), kind=kLoop, calls=%fused_computation.19 | loop fusion | flops 57344 | bytes 229376 | tf_op jit(solution)/shard_map/concatenate | solution.py:232
  2.2 14.5 %shard_map.68 = f32[9,224,128]{2,1,0:T(8,128)} custom-call(f32[224,128]{1,0:T(8,128)} %bitcast.136), custom_call_target="tpu_custom_call" | custom-call | tf_op jit(solution)/shard_map/pallas_call | solution.py:90
  16.8 1.4 %reshape.360 = f32[9,7,4096]{2,1,0:T(8,128)S(1)} reshape(f32[9,224,128]{2,1,0:T(8,128)} %shard_map.68) | data formatting | bytes 2064384 | tf_op jit(solution)/shard_map/reshape | solution.py:98
  18.2 0.2 slice.126
  18.3 0.1 copy.47
  18.4 0.1 pad_maximum_fusion.4
  18.5 1.7 %broadcast_multiply_fusion.1 = (f32[9,3,4096]{2,1,0:T(4,128)S(1)}, f32[9,3,4096]{2,1,0:T(4,128)}, f32[9,3,4096]{2,1,0:T(4,128)S(1)}, f32[9,3,4096]{2,1,0:T(4,128)}) fusion(f32[9,4096]{1,0:T(8,128)S(1)} %bitcast.131, f32[3]{0:T(128)S(1)} %pad_maximum_fusion.4, f32[9,7,4096]{2,1,0:T(8,128)S(1)} %reshape.360), kind=kLoop, calls=%fused_computation.12 | loop fusion | flops 663552 | bytes 2801676 | tf_op jit(solution)/shard_map/mul | solution.py:245
  20.2 1.1 concatenate.26.refs_2_.refs_3_
  21.3 0.0 copy-done.6
  21.4 0.1 copy.15
  21.5 0.1 add_select_fusion
  21.6 0.6 gather_fusion
  22.2 0.1 slice_select_fusion
  22.2 0.1 reshape.357
  22.4 0.1 reshape_squeeze.6
  22.5 0.7 pad_add_fusion.src_ref
  23.2 0.7 fusion.25
  23.8 0.1 broadcast_in_dim.18
  23.9 0.1 reshape.358
  24.0 0.6 pad_add_fusion.1.leaf_ref
  24.6 35.4 %shard_map.69 = (f32[32,8,128]{2,1,0:T(8,128)}, f32[32,8,128]{2,1,0:T(8,128)}) custom-call(s32[432]{0:T(512)} %pad_add_fusion.src_ref, s32[48]{0:T(128)} %pad_add_fusion.1.leaf_ref, s32[1]{0:T(128)} %bitcast.4.live_ref, f32[9,3,4096]{2,1,0:T(4,128)} %get-tuple-element.15.refs_0_, f32[9,3,4096]{2,1,0:T(4,128)} %get-tuple-element.19.refs_1_.refs_0_, ...), custom_call_target="tpu_custom_call" | custom-call | tf_op jit(solution)/shard_map/pallas_call | solution.py:194
  59.9 1.0 slice_bitcast_fusion.3
  60.9 0.7 add_divide_fusion
  61.6 0.6 fusion.24.own_ref
  62.3 10.1 %shard_map.70 = f32[9,64,128]{2,1,0:T(8,128)} custom-call(f32[64,128]{1,0:T(8,128)} %fusion.24.own_ref), custom_call_target="tpu_custom_call" | custom-call | tf_op jit(solution)/shard_map/pallas_call | solution.py:90
  72.4 1.1 reshape.361
  73.5 0.3 slice_multiply_fusion
  73.8 0.1 copy.46
  73.9 0.3 subtract_multiply_fusion.1
  74.3 1.6 %fusion.1.refs_1_ = f32[9,8,4096]{2,1,0:T(8,128)} fusion(f32[9,1,4096]{2,1,0:T(1,128)S(1)} %slice.126, f32[9,3,4096]{2,1,0:T(4,128)S(1)} %subtract_multiply_fusion.1, f32[9,1,4096]{2,1,0:T(1,128)S(1)} %get-tuple-element.17, f32[9,3,4096]{2,1,0:T(4,128)S(1)} %get-tuple-element.14), kind=kLoop, calls=%fused_computation.4 | loop fusion | flops 884736 | bytes 2359296 | tf_op jit(solution)/shard_map/concatenate | solution.py:245
  75.8 18.8 %shard_map.71 = f32[32,8,128]{2,1,0:T(8,128)} custom-call(s32[432]{0:T(512)} %pad_add_fusion.src_ref, s32[48]{0:T(128)} %pad_add_fusion.1.leaf_ref, s32[1]{0:T(128)} %bitcast.4.live_ref, f32[9,3,4096]{2,1,0:T(4,128)} %get-tuple-element.15.refs_0_, f32[9,8,4096]{2,1,0:T(8,128)} %fusion.1.refs_1_), custom_call_target="tpu_custom_call" | custom-call | tf_op jit(solution)/shard_map/pallas_call | solution.py:194
  94.6 1.0 fusion.29
  95.6 1.0 fusion.28
  96.7 0.9 slice.130
  97.6 0.0 copy-done.3
  97.6 0.6 fusion.19.own_ref
  98.2 9.5 %shard_map.72 = f32[9,96,128]{2,1,0:T(8,128)} custom-call(f32[96,128]{1,0:T(8,128)} %fusion.19.own_ref), custom_call_target="tpu_custom_call" | custom-call | tf_op jit(solution)/shard_map/pallas_call | solution.py:90
  107.8 1.1 broadcast_multiply_fusion.2
  108.9 0.2 mul.333
  109.1 0.1 copy.45
  109.2 0.3 subtract_multiply_fusion
  109.5 1.6 %fusion.3.refs_1_ = f32[9,8,4096]{2,1,0:T(8,128)} fusion(f32[9,1,4096]{2,1,0:T(1,128)S(1)} %slice.126, f32[9,3,4096]{2,1,0:T(4,128)S(1)} %subtract_multiply_fusion, f32[9,1,4096]{2,1,0:T(1,128)S(1)} %get-tuple-element.16, f32[9,3,4096]{2,1,0:T(4,128)S(1)} %get-tuple-element.18), kind=kLoop, calls=%fused_computation.6 | loop fusion | flops 884736 | bytes 2359296 | tf_op jit(solution)/shard_map/concatenate | solution.py:245
  111.0 18.8 %shard_map.73 = f32[32,8,128]{2,1,0:T(8,128)} custom-call(s32[432]{0:T(512)} %pad_add_fusion.src_ref, s32[48]{0:T(128)} %pad_add_fusion.1.leaf_ref, s32[1]{0:T(128)} %bitcast.4.live_ref, f32[9,3,4096]{2,1,0:T(4,128)} %get-tuple-element.19.refs_1_.refs_0_, f32[9,8,4096]{2,1,0:T(8,128)} %fusion.3.refs_1_), custom_call_target="tpu_custom_call" | custom-call | tf_op jit(solution)/shard_map/pallas_call | solution.py:194
  129.8 1.0 fusion.27
  130.8 0.0 copy-done.2
  130.8 1.2 copy_add_fusion
  132.0 0.7 copy.24
  132.7 0.7 copy.25
  (29 shorter events, 0.3 us)
Async XLA Ops:
  20.2 1.1 copy-start.6
  20.2 1.3 %copy-start.7 = (s32[1,1,8]{2,1,0:T(1,128)S(1)}, s32[1,1,8]{2,1,0:T(1,128)}, u32[]{:S(2)}) copy-start(s32[1,1,8]{2,1,0:T(1,128)} %param.9) | copy-start | bytes 100
  24.6 36.4 %copy-start.4 = (f32[1,1,1,4096]{3,2,1,0:T(1,128)S(1)}, f32[1,1,1,4096]{3,2,1,0:T(1,128)}, u32[]{:S(2)}) copy-start(f32[1,1,1,4096]{3,2,1,0:T(1,128)} %param.7) | copy-start | bytes 49156
  60.9 13.0 %copy-start = (f32[9,3,4096]{2,1,0:T(4,128)S(1)}, f32[9,3,4096]{2,1,0:T(4,128)}, u32[]{:S(2)}) copy-start(f32[9,3,4096]{2,1,0:T(4,128)} %get-tuple-element.15.refs_0_) | copy-start | bytes 1327108
  75.8 20.8 %copy-start.5 = (f32[2,4096]{1,0:T(2,128)S(1)}, f32[2,4096]{1,0:T(2,128)}, u32[]{:S(2)}) copy-start(f32[2,4096]{1,0:T(2,128)} %get-tuple-element.28) | copy-start | bytes 98308
  75.8 21.8 %copy-start.3 = (f32[1,1,3,4096]{3,1,2,0:T(1,128)S(1)}, f32[1,1,3,4096]{3,1,2,0:T(1,128)}, u32[]{:S(2)}) copy-start(f32[1,1,3,4096]{3,1,2,0:T(1,128)} %param.6) | copy-start | bytes 147460
  107.8 1.4 %copy-start.1 = (f32[9,3,4096]{2,1,0:T(4,128)S(1)}, f32[9,3,4096]{2,1,0:T(4,128)}, u32[]{:S(2)}) copy-start(f32[9,3,4096]{2,1,0:T(4,128)} %get-tuple-element.19.refs_1_.refs_0_) | copy-start | bytes 1327108
  111.0 19.8 %copy-start.2 = (f32[32,8,128]{2,1,0:T(8,128)S(1)}, f32[32,8,128]{2,1,0:T(8,128)}, u32[]{:S(2)}) copy-start(f32[32,8,128]{2,1,0:T(8,128)} %shard_map.71) | copy-start | bytes 393220
where the time goes:
time: 136 us; the launch traced here: 133 us
  Pallas kernels  107 us (79%)
  other arithmetic  13.7 us (10%)
  local copies, waits for them, and re-layouts  11.6 us (9%)
    pallas_call x3, Pallas kernels, all_sums(): pl.pallas_call(functools.partial(pair_sums, sections, (base_items, base_e...  72.9 us
    pallas_call x3, Pallas kernels, surround(): pl.pallas_call(functools.partial(exchange, (lax.axis_size('gx'), lax.axis...  34.2 us
    concatenate x2, other arithmetic, acceleration(): jnp.concatenate([m, m * x, mq, mq * (viscosity * v - 2.0 / kernel_scale *...  3.12 us

commit v1 on v0

v1 whole, which is shorter than its diff:
```python
import functools

import jax
import jax.numpy as jnp
from jax import lax
from jax.experimental import pallas as pl
from jax.experimental.pallas import tpu as pltpu
from jax.sharding import PartitionSpec as P

LEAF = 128
MESH = pl.DeviceIdType.MESH
BF16, F32 = jnp.bfloat16, jnp.float32

kernel_scale = 1.0
viscosity = 0.5
time_step = 0.5
base_entries = 9
COORD = (2.0 * 1.4426950408889634 / kernel_scale) ** 0.5
PUSH = 2.0 / (kernel_scale * COORD)
ABSENT = -1000.0

OWN, SIDES, CORNERS = (4,), (3, 5, 1, 7), (0, 2, 6, 8)


def rounded(value):
    return value.astype(BF16).astype(F32)


def loop(count, unroll, body):
    def several(i, carry):
        for u in range(unroll):
            body(i * unroll + u)
        return carry

    lax.fori_loop(0, count // unroll, several, 0)


def kernel(
    sizes, pos_ref, vel_ref, mass_ref, pair_ref, hot_ref, disp_ref, newv_ref,
    state, inverse, force, feature, push, target, weight_own, weight_far,
    partial, sums, rho_rows, mass_rows, mid, send_sem, recv_sem,
):
    count_x, count_y, leaves, listed, slots = sizes
    extra = listed // base_entries - 1
    tiles = leaves // 2
    gx, gy = lax.axis_index("gx"), lax.axis_index("gy")

    def inside(a, b):
        terms = []
        if a != 1:
            terms.append(gx > 0 if a == 0 else gx < count_x - 1)
        if b != 1:
            terms.append(gy > 0 if b == 0 else gy < count_y - 1)
        return terms[0] if len(terms) == 1 else terms[0] & terms[1]

    def device(a, b):
        return (jnp.clip(gx + a - 1, 0, count_x - 1), jnp.clip(gy + b - 1, 0, count_y - 1))

    def sent(buffer, number, block):
        a, b = divmod(block, 3)
        to = (1, 2 - b) if a == 1 else (2 - a, 1)
        source = 4 if a == 1 or b == 1 else 3 + b
        descriptor = pltpu.make_async_remote_copy(
            src_ref=buffer.at[source],
            dst_ref=buffer.at[block],
            send_sem=send_sem.at[number, block],
            recv_sem=recv_sem.at[number, block],
            device_id=device(*to),
            device_id_type=MESH,
        )
        return descriptor, inside(*to) if a == 1 or b == 1 else inside(2 - a, b)

    def start(buffer, number, blocks):
        for block in blocks:
            descriptor, valid = sent(buffer, number, block)
            pl.when(valid)(descriptor.start)

    def arrive(buffer, number, blocks):
        for block in blocks:
            pl.when(inside(*divmod(block, 3)))(sent(buffer, number, block)[0].wait_recv)

    messages = (state.at[0], state.at[1], inverse, force)

    row = lax.broadcasted_iota(jnp.int32, (8, LEAF), 0)
    low = row < 4
    last = row % 4 == 3
    zeros8 = jnp.zeros((8, LEAF), F32)
    ones_rows = jnp.where(row < 3, 1.0, 0.0).astype(F32)

    sides_of = ((1, 0), (1, 2), (0, 1), (2, 1))
    barrier = pltpu.get_barrier_semaphore()
    for a, b in sides_of:

        @pl.when(inside(a, b))
        def _():
            pl.semaphore_signal(barrier, inc=1, device_id=device(a, b), device_id_type=MESH)

    def span(leaf):
        return pl.ds(pl.multiple_of(leaf * LEAF, LEAF), LEAF)

    three = lax.broadcasted_iota(jnp.int32, (3, LEAF), 0)
    centre = jnp.where(
        three == 0, gx.astype(F32) + 0.5, jnp.where(three == 1, gy.astype(F32) + 0.5, 0.5)
    )

    def own_state(i):
        parts = [[], []]
        for half in range(2):
            leaf = 2 * i + half
            m = mass_ref[0, 0, :, span(leaf)]
            a1 = COORD * (pos_ref[0, 0, :, span(leaf)] - centre)
            a2 = a1 + (COORD * 0.5 * time_step) * vel_ref[0, 0, :, span(leaf)]
            mass_rows[pl.ds(leaf, 1), :] = m
            logm = jnp.log2(m)
            for section, a in enumerate((a1, a2)):
                parts[section] += [a, logm - 0.5 * jnp.sum(a * a, axis=0, keepdims=True)]
        for section in range(2):
            state[section, 4, i] = jnp.concatenate(parts[section], axis=0)

    loop(tiles, 4, own_state)
    pl.semaphore_wait(barrier, sum(inside(a, b).astype(jnp.int32) for a, b in sides_of))
    for section in range(2):
        start(messages[section], section, SIDES)

    for block in SIDES + CORNERS:

        @pl.when(jnp.logical_not(inside(*divmod(block, 3))))
        def _():
            def fill(i):
                for section in range(2):
                    state[section, block, i] = jnp.where(last, ABSENT, 0.0)
                force[block, i] = zeros8

            loop(tiles, 4, fill)
            inverse[block] = jnp.zeros((leaves, LEAF), F32)

    def paired(tile):
        hi = rounded(tile)
        lo = tile - hi
        return jnp.where(low, hi, pltpu.roll(lo, 4, 0)), jnp.where(low, pltpu.roll(hi, 4, 0), lo)

    def shifted(tile, block):
        a, b = divmod(block, 3)
        for steps, offset in ((3, a - 1), (2, b - 1)):
            if offset:
                d = COORD * offset
                coordinate = row % 4 == 3 - steps
                tile = (
                    tile
                    + jnp.where(coordinate, d, 0.0)
                    - jnp.where(last, d * pltpu.roll(tile, steps, 0) + 0.5 * d * d, 0.0)
                )
        return tile

    def prepare(section, blocks):
        for block in blocks:

            def one(i):
                halves = paired(shifted(state[section, block, i], block))
                for half in range(2):
                    feature[section, block * leaves + 2 * i + half] = jnp.concatenate(
                        [halves[half], ones_rows], axis=0
                    ).astype(BF16)

            loop(tiles, 4, one)

    def prepare_target(section):
        def one(i):
            tile = state[section, 4, i]
            hi = rounded(tile)
            lo = tile - hi
            square = tile * tile
            for half in range(2):
                if half == 0:
                    h, l = jnp.where(low, hi, pltpu.roll(hi, 4, 0)), jnp.where(low, lo, pltpu.roll(lo, 4, 0))
                else:
                    h, l = jnp.where(low, pltpu.roll(hi, 4, 0), hi), jnp.where(low, pltpu.roll(lo, 4, 0), lo)
                mine = (row // 4 == half) & jnp.logical_not(last)
                c = -0.5 * jnp.sum(jnp.where(mine, square, 0.0), axis=0, keepdims=True)
                c1 = rounded(c)
                c2 = rounded(c - c1)
                c3 = c - c1 - c2
                crows = jnp.where(row == 0, c1, jnp.where(row == 1, c2, jnp.where(row == 2, c3, 0.0)))
                stack = jnp.concatenate(
                    [jnp.where(last, 1.0, h), crows, jnp.where(last, 0.0, l), zeros8]
                    + [jnp.zeros((LEAF - 32, LEAF), F32)],
                    axis=0,
                )
                target[section, 2 * i + half] = stack.T.astype(BF16)

        loop(tiles, 2, one)

    def source(leaf, entry, block):
        return block * leaves + pair_ref[0, 0, leaf, entry] % leaves

    def slot_leaf(slot):
        return jnp.minimum(hot_ref[0, 0, slot], leaves - 1)

    def weigh(section, leaf, blocks, offsets, store):
        near = jnp.concatenate(
            [
                feature[section, source(leaf, offset + block, block)]
                for offset in offsets
                for block in blocks
            ],
            axis=1,
        )
        exponent = jnp.dot(
            target[section, leaf][:, 0:32],
            jnp.concatenate([near, near], axis=0),
            preferred_element_type=F32,
        )
        weight = jnp.exp2(exponent)
        store(weight.astype(BF16))
        pieces = [weight[:, k * LEAF : (k + 1) * LEAF] for k in range(weight.shape[1] // LEAF)]
        return functools.reduce(jnp.add, pieces)

    def hot_offsets(e):
        return (base_entries * (1 + e),)

    def keep(ref, index):
        def store(value):
            ref[index] = value

        return store

    def density(section, group):
        first = group is OWN
        final = group is CORNERS
        store_own = weight_own.at[section]
        store_far = weight_far.at[section, 0 if group is SIDES else 1]

        def finish(index, value):
            if not first:
                value = value + partial[index]
            if final:
                rho_rows[pl.ds(index, 1), :] = jnp.sum(value.T, axis=0, keepdims=True)
            else:
                partial[index] = value

        def base(i):
            ref = store_own.at[i, :, 0:LEAF] if first else store_far.at[i]
            finish(i, weigh(section, i, group, (0,), keep(ref, ...)))

        loop(leaves, 8 if not first else 8, base)

        def hot(s):
            leaf = slot_leaf(s)
            if first:
                offsets = tuple(base_entries * (1 + e) for e in range(extra))
                value = weigh(section, leaf, group, offsets, keep(store_own.at[leaves + s], ...))
            else:
                value = functools.reduce(
                    jnp.add,
                    [
                        weigh(
                            section, leaf, group, (base_entries * (1 + e),),
                            keep(store_far.at[leaves + extra * s + e], ...),
                        )
                        for e in range(extra)
                    ],
                )
            finish(leaves + s, value)

        loop(slots, 4, hot)

    def inverse_density():
        total = mass_rows[...] + rho_rows[pl.ds(0, leaves), :]
        leaf = lax.broadcasted_iota(jnp.int32, (leaves, LEAF), 0)
        for s in range(slots):
            total = total + jnp.where(leaf == hot_ref[0, 0, s], rho_rows[pl.ds(leaves + s, 1), :], 0.0)
        return 1.0 / total

    def store_push(block, i, tile):
        halves = paired(tile)
        for half in range(2):
            push[block * leaves + 2 * i + half] = jnp.concatenate(
                [halves[half], zeros8], axis=0
            ).astype(BF16)

    def spread(rows, i, block):
        first = jnp.broadcast_to(rows[block, pl.ds(2 * i, 1), :], (8, LEAF))
        second = jnp.broadcast_to(rows[block, pl.ds(2 * i + 1, 1), :], (8, LEAF))
        return jnp.where(low, first, second)

    def drive(tile, velocity, q):
        return q * jnp.where(last, 1.0, viscosity * velocity - PUSH * tile)

    def prepare_push1(blocks):
        for block in blocks:

            def one(i):
                here = state[0, block, i]
                velocity = (state[1, block, i] - here) * (1.0 / (COORD * 0.5 * time_step))
                store_push(
                    block, i, drive(shifted(here, block), velocity, spread(inverse, i, block))
                )

            loop(tiles, 4, one)

    def prepare_push2(blocks):
        for block in blocks:
            a, b = divmod(block, 3)

            def one(i):
                tile = force[block, i]
                for steps, offset in ((5, a - 1), (6, b - 1)):
                    if offset:
                        tile = tile - jnp.where(
                            row % 4 == steps - 5,
                            (2.0 / kernel_scale) * offset * pltpu.roll(tile, steps, 0),
                            0.0,
                        )
                store_push(block, i, tile)

            loop(tiles, 4, one)

    def gather(section, leaf, blocks, offsets, weight):
        near = []
        for offset in offsets:
            for block in blocks:
                index = source(leaf, offset + block, block)
                near.append(jnp.concatenate([feature[section, index], push[index]], axis=0))
        return lax.dot_general(
            weight, jnp.concatenate(near, axis=1), (((1,), (1,)), ((), ())),
            preferred_element_type=F32,
        )

    def accumulate(section, group):
        first = group is OWN
        load_own = weight_own.at[section]
        load_far = weight_far.at[section, 0 if group is SIDES else 1]

        def finish(index, value):
            sums[index] = value if first else sums[index] + value

        def base(i):
            weight = load_own[i, :, 0:LEAF] if first else load_far[i]
            finish(i, gather(section, i, group, (0,), weight))

        loop(leaves, 8, base)

        def hot(s):
            leaf = slot_leaf(s)
            if first:
                offsets = tuple(base_entries * (1 + e) for e in range(extra))
                value = gather(section, leaf, group, offsets, load_own[leaves + s])
            else:
                value = functools.reduce(
                    jnp.add,
                    [
                        gather(
                            section, leaf, group, (base_entries * (1 + e),),
                            load_far[leaves + extra * s + e],
                        )
                        for e in range(extra)
                    ],
                )
            finish(leaves + s, value)

        loop(slots, 4, hot)

    def combined(index):
        rows = sums[index].T
        near, pressed = rows[0:8], rows[16:24]
        near = near + pltpu.roll(near, 4, 0)
        near = jnp.where(last, jnp.broadcast_to(rows[8:9], (8, LEAF)), near)
        pressed = pressed + pltpu.roll(pressed, 4, 0)
        return jnp.where(low, near, pressed)

    def collect():
        def hot(s):
            rho_hot[s] = combined(leaves + s)

        loop(slots, 4, hot)

    rho_hot = mid.at[1]

    def accelerations(section, use):
        collect()

        def one(leaf):
            total = combined(leaf)
            for s in range(slots):
                mine = (hot_ref[0, 0, s] == leaf).astype(F32)
                total = total + mine * rho_hot[s]
            use(leaf, total)

        loop(leaves, 4, one)

    def acceleration(section, leaf, total, q, velocity):
        i, half = leaf // 2, leaf % 2
        a = state[section, 4, i, pl.ds(4 * half, 3), :]
        sq = total[7:8]
        return (
            PUSH * (q * (a * total[3:4] - total[0:3]) + a * sq)
            + total[4:7]
            - viscosity * velocity * sq
        )

    prepare_target(0)
    prepare(0, OWN)
    density(0, OWN)
    arrive(messages[0], 0, (3, 5))
    start(messages[0], 0, CORNERS)
    prepare_target(1)
    arrive(messages[0], 0, (1, 7))
    prepare(0, SIDES)
    density(0, SIDES)
    arrive(messages[1], 1, (3, 5))
    start(messages[1], 1, CORNERS)
    prepare(1, OWN)
    arrive(messages[0], 0, CORNERS)
    prepare(0, CORNERS)
    density(0, CORNERS)
    inverse[4] = inverse_density()
    start(inverse, 2, SIDES)

    density(1, OWN)
    arrive(messages[1], 1, (1, 7))
    prepare(1, SIDES)
    density(1, SIDES)
    arrive(inverse, 2, (3, 5))
    start(inverse, 2, CORNERS)
    arrive(messages[1], 1, CORNERS)
    prepare(1, CORNERS)
    density(1, CORNERS)
    rho_rows[pl.ds(0, leaves), :] = inverse_density()

    prepare_push1(OWN)
    accumulate(0, OWN)
    arrive(inverse, 2, (1, 7))
    prepare_push1(SIDES)
    accumulate(0, SIDES)
    arrive(inverse, 2, CORNERS)
    prepare_push1(CORNERS)
    accumulate(0, CORNERS)

    def use1(leaf, total):
        velocity = vel_ref[0, 0, :, span(leaf)]
        q = inverse[4, pl.ds(leaf, 1), :]
        moved = velocity + 0.5 * time_step * acceleration(0, leaf, total, q, velocity)
        mid[0, leaf, 0:3] = moved
        disp_ref[0, 0, :, span(leaf)] = time_step * moved

    accelerations(0, use1)

    def own_force(i):
        parts = []
        for half in range(2):
            leaf = 2 * i + half
            q = rho_rows[pl.ds(leaf, 1), :]
            a = state[1, 4, i, pl.ds(4 * half, 3), :]
            parts += [q * (viscosity * mid[0, leaf, 0:3] - PUSH * a), q]
        force[4, i] = jnp.concatenate(parts, axis=0)

    loop(tiles, 4, own_force)
    start(force, 3, SIDES)
    prepare_push2(OWN)
    accumulate(1, OWN)
    arrive(force, 3, (3, 5))
    start(force, 3, CORNERS)
    arrive(force, 3, (1, 7))
    prepare_push2(SIDES)
    accumulate(1, SIDES)
    arrive(force, 3, CORNERS)
    prepare_push2(CORNERS)
    accumulate(1, CORNERS)

    def use2(leaf, total):
        q = rho_rows[pl.ds(leaf, 1), :]
        acc = acceleration(1, leaf, total, q, mid[0, leaf, 0:3])
        newv_ref[0, 0, :, span(leaf)] = vel_ref[0, 0, :, span(leaf)] + time_step * acc

    accelerations(1, use2)

    for number, buffer in enumerate(messages):
        for block in SIDES + CORNERS:
            descriptor, valid = sent(buffer, number, block)
            pl.when(valid)(descriptor.wait_send)


def local(position, velocity, mass, pair_list, hot_leaf):
    leaves, listed = pair_list.shape[2:]
    slots = hot_leaf.shape[2]
    extra = listed // base_entries - 1
    sizes = (lax.axis_size("gx"), lax.axis_size("gy"), leaves, listed, slots)
    vmem = pl.BlockSpec(memory_space=pltpu.VMEM)
    smem = pl.BlockSpec(memory_space=pltpu.SMEM)
    shape = jax.ShapeDtypeStruct(position.shape, F32)
    tiles = leaves // 2
    return pl.pallas_call(
        functools.partial(kernel, sizes),
        out_shape=[shape, shape],
        in_specs=[vmem] * 3 + [smem] * 2,
        out_specs=[vmem] * 2,
        scratch_shapes=[
            pltpu.VMEM((2, 9, tiles, 8, LEAF), F32),
            pltpu.VMEM((9, leaves, LEAF), F32),
            pltpu.VMEM((9, tiles, 8, LEAF), F32),
            pltpu.VMEM((2, 9 * leaves, 16, LEAF), BF16),
            pltpu.VMEM((9 * leaves, 16, LEAF), BF16),
            pltpu.VMEM((2, leaves, LEAF, LEAF), BF16),
            pltpu.VMEM((2, leaves + slots, LEAF, extra * LEAF), BF16),
            pltpu.VMEM((2, 2, leaves + extra * slots, LEAF, 4 * LEAF), BF16),
            pltpu.VMEM((leaves + slots, LEAF, LEAF), F32),
            pltpu.VMEM((leaves + slots, LEAF, 32), F32),
            pltpu.VMEM((leaves + slots, LEAF), F32),
            pltpu.VMEM((leaves, LEAF), F32),
            pltpu.VMEM((2, leaves, 8, LEAF), F32),
            pltpu.SemaphoreType.DMA((4, 9)),
            pltpu.SemaphoreType.DMA((4, 9)),
        ],
        compiler_params=pltpu.CompilerParams(
            collective_id=0, has_side_effects=True, vmem_limit_bytes=60 * 2**20
        ),
    )(position, velocity, mass, pair_list, hot_leaf)


def solution(mesh):
    return jax.shard_map(
        local,
        mesh=mesh,
        in_specs=(
            P("gx", "gy", None, None),
            P("gx", "gy", None, None),
            P("gx", "gy", None, None),
            P("gx", "gy", None, None),
            P("gx", "gy", None),
        ),
        out_specs=(P("gx", "gy", None, None), P("gx", "gy", None, None)),
        check_vma=False,
    )
```

time: 136 us -> 53.3 us (0.39); the launches traced: 133 us -> 52.8 us
  Pallas kernels: 107 us -> 46.5 us
  other arithmetic: 13.7 us -> 0 us
  local copies, waits for them, and re-layouts: 11.6 us -> 5.73 us
    pallas_call x6 -> x1, Pallas kernels: 107 us -> 46.5 us  [local(): pl.pallas_call(functools.partial(kernel, sizes), out_shape=[shape, shape]...]
    concatenate x5 -> x0, other arithmetic: 5.98 us -> none  [the longest x2 3.12 us: acceleration(): jnp.concatenate([m, m * x, mq, mq * (viscosity * v - 2.0 / kernel_scale *...]
    slice x10 -> x0, local copies, waits for them, and re-layouts: 5.09 us -> none  [the longest x2 2.01 us: acceleration(): s[0:1]]
    mul x9 -> x0, other arithmetic: 3.71 us -> none  [the longest x1 1.68 us: acceleration(): m * x]
    reshape x4 -> x0, local copies, waits for them, and re-layouts: 2.67 us -> none  [the longest x2 2.5 us: surround(): return out.reshape(9, channels, width)]
    pallas_call x0 -> x2, local copies, waits for them, and re-layouts: none -> 2.21 us  [local(): pl.pallas_call(functools.partial(kernel, sizes), out_shape=[shape, shape]...]
    unnamed x21 -> x7, local copies, waits for them, and re-layouts: 1.64 us -> 3.52 us
    add x2 -> x0, other arithmetic: 1.8 us -> none  [the longest x1 1.15 us: local(): own_v + time_step * acc2]
where the time goes in v1:
time: 53.3 us; the launch traced here: 52.8 us
  Pallas kernels  46.5 us (87%)
  local copies, waits for them, and re-layouts  5.73 us (11%)
  between operations  0.65 us (1%)
    pallas_call x1, Pallas kernels, local(): pl.pallas_call(functools.partial(kernel, sizes), out_shape=[shape, shape]...  46.5 us
    unnamed x7, local copies, waits for them, and re-layouts  3.52 us
    pallas_call x2, local copies, waits for them, and re-layouts, local(): pl.pallas_call(functools.partial(kernel, sizes), out_shape=[shape, shape]...  2.21 us

profile of v1, /device:TPU:17, one launch (start us, length us, event | category | flops | bytes accessed | tf_op | source)
XLA Modules:
  0.0 52.8 jit_solution(4104318490824103933)
XLA Ops:
  0.6 1.4 %copy.9.pair_ref = s32[1,1,32,27]{3,2,1,0:T(8,128)} copy(s32[1,1,32,27]{2,1,3,0:T(1,128)} %param.8) | data formatting | bytes 6912 | tf_op args[3]
  2.0 0.0 copy-start.1
  2.0 1.5 %copy.7.pos_ref = f32[1,1,3,4096]{3,2,1,0:T(4,128)} copy(f32[1,1,3,4096]{3,1,2,0:T(1,128)} %param.5) | data formatting | bytes 98304 | tf_op args[0]
  3.5 0.0 copy-done.1
  3.5 0.7 %copy.8.vel_ref = f32[1,1,3,4096]{3,2,1,0:T(4,128)} copy(f32[1,1,3,4096]{3,1,2,0:T(1,128)S(1)} %copy-done.1) | data formatting | bytes 98304 | tf_op args[1]
  4.1 46.5 %shard_map.68 = (f32[1,1,3,4096]{3,2,1,0:T(4,128)}, f32[1,1,3,4096]{3,2,1,0:T(4,128)}) custom-call(f32[1,1,3,4096]{3,2,1,0:T(4,128)} %copy.7.pos_ref, f32[1,1,3,4096]{3,2,1,0:T(4,128)} %copy.8.vel_ref, f32[1,1,1,4096]{3,2,1,0:T(1,128)} %mass_ref.1, s32[1,1,32,27]{3,2,1,0:T(8,128)} %copy.9.pair_ref, s32[1,1,8]{2,1,0:T(1,128)} %hot_ref.1), custom_call_target="tpu_custom_call" | custom-call | tf_op jit(solution)/shard_map/pallas_call | solution.py:492
  50.6 0.0 copy-start
  50.6 1.5 %copy.10 = f32[1,1,3,4096]{3,1,2,0:T(1,128)} copy(f32[1,1,3,4096]{3,2,1,0:T(4,128)} %get-tuple-element.2) | data formatting | bytes 98304 | tf_op jit(solution)/shard_map/pallas_call | solution.py:492
  52.2 0.0 copy-done
  52.2 0.7 %copy.11 = f32[1,1,3,4096]{3,1,2,0:T(1,128)} copy(f32[1,1,3,4096]{3,2,1,0:T(4,128)S(1)} %copy-done) | data formatting | bytes 98304 | tf_op jit(solution)/shard_map/pallas_call | solution.py:492
Async XLA Ops:
  2.0 1.5 %copy-start.1 = (f32[1,1,3,4096]{3,1,2,0:T(1,128)S(1)}, f32[1,1,3,4096]{3,1,2,0:T(1,128)}, u32[]{:S(2)}) copy-start(f32[1,1,3,4096]{3,1,2,0:T(1,128)} %param.6) | copy-start | bytes 147460
  50.6 1.6 %copy-start = (f32[1,1,3,4096]{3,2,1,0:T(4,128)S(1)}, f32[1,1,3,4096]{3,2,1,0:T(4,128)}, u32[]{:S(2)}) copy-start(f32[1,1,3,4096]{3,2,1,0:T(4,128)} %get-tuple-element.3) | copy-start | bytes 147460

commit v2 on v1

--- a/solution.py
+++ b/solution.py
@@ -18,6 +18,7 @@
 COORD = (2.0 * 1.4426950408889634 / kernel_scale) ** 0.5
 PUSH = 2.0 / (kernel_scale * COORD)
 ABSENT = -1000.0
+CHANNELS = 24
 
 OWN, SIDES, CORNERS = (4,), (3, 5, 1, 7), (0, 2, 6, 8)
 
@@ -38,7 +39,7 @@
 def kernel(
     sizes, pos_ref, vel_ref, mass_ref, pair_ref, hot_ref, disp_ref, newv_ref,
     state, inverse, force, feature, push, target, weight_own, weight_far,
-    partial, sums, rho_rows, mass_rows, mid, send_sem, recv_sem,
+    partial, sums, rho_rows, mid, send_sem, recv_sem,
 ):
     count_x, count_y, leaves, listed, slots = sizes
     extra = listed // base_entries - 1
@@ -95,29 +96,24 @@
         def _():
             pl.semaphore_signal(barrier, inc=1, device_id=device(a, b), device_id_type=MESH)
 
-    def span(leaf):
-        return pl.ds(pl.multiple_of(leaf * LEAF, LEAF), LEAF)
-
-    three = lax.broadcasted_iota(jnp.int32, (3, LEAF), 0)
-    centre = jnp.where(
-        three == 0, gx.astype(F32) + 0.5, jnp.where(three == 1, gy.astype(F32) + 0.5, 0.5)
-    )
-
-    def own_state(i):
-        parts = [[], []]
-        for half in range(2):
-            leaf = 2 * i + half
-            m = mass_ref[0, 0, :, span(leaf)]
-            a1 = COORD * (pos_ref[0, 0, :, span(leaf)] - centre)
-            a2 = a1 + (COORD * 0.5 * time_step) * vel_ref[0, 0, :, span(leaf)]
-            mass_rows[pl.ds(leaf, 1), :] = m
-            logm = jnp.log2(m)
-            for section, a in enumerate((a1, a2)):
-                parts[section] += [a, logm - 0.5 * jnp.sum(a * a, axis=0, keepdims=True)]
-        for section in range(2):
-            state[section, 4, i] = jnp.concatenate(parts[section], axis=0)
-
-    loop(tiles, 4, own_state)
+    def lanes(component, pitch=4, count=leaves):
+        return pl.ds(component, count, stride=pitch)
+
+    centre = (gx.astype(F32) + 0.5, gy.astype(F32) + 0.5, 0.5)
+
+    def own_state():
+        logm = jnp.log2(mass_ref[...])
+        first = [COORD * (pos_ref[d] - centre[d]) for d in range(3)]
+        second = [first[d] + (COORD * 0.5 * time_step) * vel_ref[d] for d in range(3)]
+        for section, a in enumerate((first, second)):
+            for d in range(3):
+                state[section, 4, lanes(d), :] = a[d]
+            state[section, 4, lanes(3), :] = logm - 0.5 * (a[0] * a[0] + a[1] * a[1] + a[2] * a[2])
+
+    def tile_rows(i):
+        return pl.ds(pl.multiple_of(8 * i, 8), 8)
+
+    own_state()
     pl.semaphore_wait(barrier, sum(inside(a, b).astype(jnp.int32) for a, b in sides_of))
     for section in range(2):
         start(messages[section], section, SIDES)
@@ -128,8 +124,8 @@
         def _():
             def fill(i):
                 for section in range(2):
-                    state[section, block, i] = jnp.where(last, ABSENT, 0.0)
-                force[block, i] = zeros8
+                    state[section, block, tile_rows(i), :] = jnp.where(last, ABSENT, 0.0)
+                force[block, tile_rows(i), :] = zeros8
 
             loop(tiles, 4, fill)
             inverse[block] = jnp.zeros((leaves, LEAF), F32)
@@ -156,17 +152,17 @@
         for block in blocks:
 
             def one(i):
-                halves = paired(shifted(state[section, block, i], block))
+                halves = paired(shifted(state[section, block, tile_rows(i), :], block))
                 for half in range(2):
                     feature[section, block * leaves + 2 * i + half] = jnp.concatenate(
                         [halves[half], ones_rows], axis=0
                     ).astype(BF16)
 
-            loop(tiles, 4, one)
+            loop(tiles, 8, one)
 
     def prepare_target(section):
         def one(i):
-            tile = state[section, 4, i]
+            tile = state[section, 4, tile_rows(i), :]
             hi = rounded(tile)
             lo = tile - hi
             square = tile * tile
@@ -188,10 +184,10 @@
                 )
                 target[section, 2 * i + half] = stack.T.astype(BF16)
 
-        loop(tiles, 2, one)
-
-    def source(leaf, entry, block):
-        return block * leaves + pair_ref[0, 0, leaf, entry] % leaves
+        loop(tiles, 4, one)
+
+    def source(leaf, entry):
+        return pair_ref[0, entry, 0, leaf]
 
     def slot_leaf(slot):
         return jnp.minimum(hot_ref[0, 0, slot], leaves - 1)
@@ -199,7 +195,7 @@
     def weigh(section, leaf, blocks, offsets, store):
         near = jnp.concatenate(
             [
-                feature[section, source(leaf, offset + block, block)]
+                feature[section, source(leaf, offset + block)]
                 for offset in offsets
                 for block in blocks
             ],
@@ -242,7 +238,7 @@
             ref = store_own.at[i, :, 0:LEAF] if first else store_far.at[i]
             finish(i, weigh(section, i, group, (0,), keep(ref, ...)))
 
-        loop(leaves, 8 if not first else 8, base)
+        loop(leaves, 16, base)
 
         def hot(s):
             leaf = slot_leaf(s)
@@ -265,7 +261,7 @@
         loop(slots, 4, hot)
 
     def inverse_density():
-        total = mass_rows[...] + rho_rows[pl.ds(0, leaves), :]
+        total = mass_ref[...] + rho_rows[pl.ds(0, leaves), :]
         leaf = lax.broadcasted_iota(jnp.int32, (leaves, LEAF), 0)
         for s in range(slots):
             total = total + jnp.where(leaf == hot_ref[0, 0, s], rho_rows[pl.ds(leaves + s, 1), :], 0.0)
@@ -290,8 +286,8 @@
         for block in blocks:
 
             def one(i):
-                here = state[0, block, i]
-                velocity = (state[1, block, i] - here) * (1.0 / (COORD * 0.5 * time_step))
+                here = state[0, block, tile_rows(i), :]
+                velocity = (state[1, block, tile_rows(i), :] - here) * (1.0 / (COORD * 0.5 * time_step))
                 store_push(
                     block, i, drive(shifted(here, block), velocity, spread(inverse, i, block))
                 )
@@ -303,7 +299,7 @@
             a, b = divmod(block, 3)
 
             def one(i):
-                tile = force[block, i]
+                tile = force[block, tile_rows(i), :]
                 for steps, offset in ((5, a - 1), (6, b - 1)):
                     if offset:
                         tile = tile - jnp.where(
@@ -319,12 +315,12 @@
         near = []
         for offset in offsets:
             for block in blocks:
-                index = source(leaf, offset + block, block)
+                index = source(leaf, offset + block)
                 near.append(jnp.concatenate([feature[section, index], push[index]], axis=0))
         return lax.dot_general(
-            weight, jnp.concatenate(near, axis=1), (((1,), (1,)), ((), ())),
+            jnp.concatenate(near, axis=1), weight, (((1,), (1,)), ((), ())),
             preferred_element_type=F32,
-        )
+        )[0:CHANNELS]
 
     def accumulate(section, group):
         first = group is OWN
@@ -332,13 +328,14 @@
         load_far = weight_far.at[section, 0 if group is SIDES else 1]
 
         def finish(index, value):
-            sums[index] = value if first else sums[index] + value
+            rows = pl.ds(pl.multiple_of(CHANNELS * index, 8), CHANNELS)
+            sums[rows, :] = value if first else sums[rows, :] + value
 
         def base(i):
             weight = load_own[i, :, 0:LEAF] if first else load_far[i]
             finish(i, gather(section, i, group, (0,), weight))
 
-        loop(leaves, 8, base)
+        loop(leaves, 16, base)
 
         def hot(s):
             leaf = slot_leaf(s)
@@ -360,43 +357,29 @@
 
         loop(slots, 4, hot)
 
-    def combined(index):
-        rows = sums[index].T
-        near, pressed = rows[0:8], rows[16:24]
-        near = near + pltpu.roll(near, 4, 0)
-        near = jnp.where(last, jnp.broadcast_to(rows[8:9], (8, LEAF)), near)
-        pressed = pressed + pltpu.roll(pressed, 4, 0)
-        return jnp.where(low, near, pressed)
-
-    def collect():
-        def hot(s):
-            rho_hot[s] = combined(leaves + s)
-
-        loop(slots, 4, hot)
-
-    rho_hot = mid.at[1]
-
-    def accelerations(section, use):
-        collect()
-
-        def one(leaf):
-            total = combined(leaf)
+    def acceleration(section, q, velocity):
+        leaf = lax.broadcasted_iota(jnp.int32, (leaves, LEAF), 0)
+        mine = [leaf == hot_ref[0, 0, s] for s in range(slots)]
+
+        def channel(*rows):
+            both = functools.reduce(
+                jnp.add, [sums[lanes(r, CHANNELS, leaves + slots), :] for r in rows]
+            )
+            total = both[0:leaves]
             for s in range(slots):
-                mine = (hot_ref[0, 0, s] == leaf).astype(F32)
-                total = total + mine * rho_hot[s]
-            use(leaf, total)
-
-        loop(leaves, 4, one)
-
-    def acceleration(section, leaf, total, q, velocity):
-        i, half = leaf // 2, leaf % 2
-        a = state[section, 4, i, pl.ds(4 * half, 3), :]
-        sq = total[7:8]
-        return (
-            PUSH * (q * (a * total[3:4] - total[0:3]) + a * sq)
-            + total[4:7]
-            - viscosity * velocity * sq
-        )
+                total = total + jnp.where(mine[s], both[leaves + s : leaves + s + 1], 0.0)
+            return total
+
+        s1, sq = channel(8), channel(19, 23)
+        result = []
+        for d in range(3):
+            a = state[section, 4, lanes(d), :]
+            result.append(
+                PUSH * (q * (a * s1 - channel(d, d + 4)) + a * sq)
+                + channel(16 + d, 20 + d)
+                - viscosity * velocity[d] * sq
+            )
+        return result
 
     prepare_target(0)
     prepare(0, OWN)
@@ -436,25 +419,15 @@
     prepare_push1(CORNERS)
     accumulate(0, CORNERS)
 
-    def use1(leaf, total):
-        velocity = vel_ref[0, 0, :, span(leaf)]
-        q = inverse[4, pl.ds(leaf, 1), :]
-        moved = velocity + 0.5 * time_step * acceleration(0, leaf, total, q, velocity)
-        mid[0, leaf, 0:3] = moved
-        disp_ref[0, 0, :, span(leaf)] = time_step * moved
-
-    accelerations(0, use1)
-
-    def own_force(i):
-        parts = []
-        for half in range(2):
-            leaf = 2 * i + half
-            q = rho_rows[pl.ds(leaf, 1), :]
-            a = state[1, 4, i, pl.ds(4 * half, 3), :]
-            parts += [q * (viscosity * mid[0, leaf, 0:3] - PUSH * a), q]
-        force[4, i] = jnp.concatenate(parts, axis=0)
-
-    loop(tiles, 4, own_force)
+    velocity = [vel_ref[d] for d in range(3)]
+    acc = acceleration(0, inverse[4], velocity)
+    moved = [velocity[d] + 0.5 * time_step * acc[d] for d in range(3)]
+    q = rho_rows[pl.ds(0, leaves), :]
+    for d in range(3):
+        force[4, lanes(d), :] = q * (viscosity * moved[d] - PUSH * state[1, 4, lanes(d), :])
+        mid[d] = moved[d]
+        disp_ref[d] = time_step * moved[d]
+    force[4, lanes(3), :] = q
     start(force, 3, SIDES)
     prepare_push2(OWN)
     accumulate(1, OWN)
@@ -467,12 +440,9 @@
     prepare_push2(CORNERS)
     accumulate(1, CORNERS)
 
-    def use2(leaf, total):
-        q = rho_rows[pl.ds(leaf, 1), :]
-        acc = acceleration(1, leaf, total, q, mid[0, leaf, 0:3])
-        newv_ref[0, 0, :, span(leaf)] = vel_ref[0, 0, :, span(leaf)] + time_step * acc
-
-    accelerations(1, use2)
+    acc = acceleration(1, rho_rows[pl.ds(0, leaves), :], [mid[d] for d in range(3)])
+    for d in range(3):
+        newv_ref[d] = vel_ref[d] + time_step * acc[d]
 
     for number, buffer in enumerate(messages):
         for block in SIDES + CORNERS:
@@ -487,34 +457,39 @@
     sizes = (lax.axis_size("gx"), lax.axis_size("gy"), leaves, listed, slots)
     vmem = pl.BlockSpec(memory_space=pltpu.VMEM)
     smem = pl.BlockSpec(memory_space=pltpu.SMEM)
-    shape = jax.ShapeDtypeStruct(position.shape, F32)
-    tiles = leaves // 2
-    return pl.pallas_call(
+    shape = jax.ShapeDtypeStruct((3, leaves, LEAF), F32)
+    outs = pl.pallas_call(
         functools.partial(kernel, sizes),
         out_shape=[shape, shape],
         in_specs=[vmem] * 3 + [smem] * 2,
         out_specs=[vmem] * 2,
         scratch_shapes=[
-            pltpu.VMEM((2, 9, tiles, 8, LEAF), F32),
+            pltpu.VMEM((2, 9, 4 * leaves, LEAF), F32),
             pltpu.VMEM((9, leaves, LEAF), F32),
-            pltpu.VMEM((9, tiles, 8, LEAF), F32),
+            pltpu.VMEM((9, 4 * leaves, LEAF), F32),
             pltpu.VMEM((2, 9 * leaves, 16, LEAF), BF16),
             pltpu.VMEM((9 * leaves, 16, LEAF), BF16),
             pltpu.VMEM((2, leaves, LEAF, LEAF), BF16),
             pltpu.VMEM((2, leaves + slots, LEAF, extra * LEAF), BF16),
             pltpu.VMEM((2, 2, leaves + extra * slots, LEAF, 4 * LEAF), BF16),
             pltpu.VMEM((leaves + slots, LEAF, LEAF), F32),
-            pltpu.VMEM((leaves + slots, LEAF, 32), F32),
+            pltpu.VMEM(((leaves + slots) * CHANNELS, LEAF), F32),
             pltpu.VMEM((leaves + slots, LEAF), F32),
-            pltpu.VMEM((leaves, LEAF), F32),
-            pltpu.VMEM((2, leaves, 8, LEAF), F32),
+            pltpu.VMEM((3, leaves, LEAF), F32),
             pltpu.SemaphoreType.DMA((4, 9)),
             pltpu.SemaphoreType.DMA((4, 9)),
         ],
         compiler_params=pltpu.CompilerParams(
             collective_id=0, has_side_effects=True, vmem_limit_bytes=60 * 2**20
         ),
-    )(position, velocity, mass, pair_list, hot_leaf)
+    )(
+        position.reshape(3, leaves, LEAF),
+        velocity.reshape(3, leaves, LEAF),
+        mass.reshape(leaves, LEAF),
+        jnp.transpose(pair_list, (0, 3, 1, 2)),
+        hot_leaf,
+    )
+    return tuple(out.reshape(position.shape) for out in outs)
 
 
 def solution(mesh):

time: 53.3 us -> 44.6 us (0.84)
  Pallas kernels: 46.5 us -> 41.7 us
  local copies, waits for them, and re-layouts: 5.73 us -> 2.06 us
    pallas_call x1, Pallas kernels: 46.5 us -> 41.7 us  [local(): pl.pallas_call(functools.partial(kernel, sizes), out_shape=[shape, shape]...]
    pallas_call x2 -> x0, local copies, waits for them, and re-layouts: 2.21 us -> none  [local(): pl.pallas_call(functools.partial(kernel, sizes), out_shape=[shape, shape]...]
    unnamed x7 -> x4, local copies, waits for them, and re-layouts: 3.52 us -> 2.06 us
where the time goes in v2:
time: 44.6 us; the launch traced here: 44.4 us
  Pallas kernels  41.7 us (93%)
  local copies, waits for them, and re-layouts  2.06 us (5%)
  between operations  0.65 us (1%)
    pallas_call x1, Pallas kernels, local(): pl.pallas_call(functools.partial(kernel, sizes), out_shape=[shape, shape]...  41.7 us
    unnamed x4, local copies, waits for them, and re-layouts  2.06 us

profile of v2, /device:TPU:17, one launch (start us, length us, event | category | flops | bytes accessed | tf_op | source)
XLA Modules:
  0.0 44.4 jit_solution(15757545718610065541)
XLA Ops:
  0.6 41.7 %shard_map.68 = (f32[3,32,128]{2,1,0:T(8,128)}, f32[3,32,128]{2,1,0:T(8,128)}) custom-call(f32[3,32,128]{2,1,0:T(8,128)} %bitcast.8, f32[3,32,128]{2,1,0:T(8,128)} %bitcast.9, f32[32,128]{1,0:T(8,128)} %bitcast.10, s32[1,27,1,32]{3,2,1,0:T(1,128)} %bitcast.11, s32[1,1,8]{2,1,0:T(1,128)} %hot_ref.1), custom_call_target="tpu_custom_call" | custom-call | tf_op jit(solution)/shard_map/pallas_call | solution.py:461
  42.3 0.0 copy-start
  42.3 1.4 %copy.13 = f32[1,1,3,4096]{3,1,2,0:T(1,128)} copy(f32[1,1,3,4096]{3,1,2,0:T(1,128)} %bitcast.7) | data formatting | bytes 98304
  43.8 0.0 copy-done
  43.8 0.6 %copy.14 = f32[1,1,3,4096]{3,1,2,0:T(1,128)} copy(f32[1,1,3,4096]{3,1,2,0:T(1,128)S(1)} %bitcast.6) | data formatting | bytes 98304
Async XLA Ops:
  42.3 1.4 %copy-start = (f32[3,32,128]{2,1,0:T(8,128)S(1)}, f32[3,32,128]{2,1,0:T(8,128)}, u32[]{:S(2)}) copy-start(f32[3,32,128]{2,1,0:T(8,128)} %get-tuple-element.5) | copy-start | bytes 147460

commit v3 on v2

--- a/solution.py
+++ b/solution.py
@@ -33,13 +33,17 @@
             body(i * unroll + u)
         return carry
 
-    lax.fori_loop(0, count // unroll, several, 0)
+    if count == unroll:
+        several(0, 0)
+    else:
+        lax.fori_loop(0, count // unroll, several, 0)
 
 
 def kernel(
-    sizes, pos_ref, vel_ref, mass_ref, pair_ref, hot_ref, disp_ref, newv_ref,
+    sizes, pos_in, vel_in, mass_in, pair_in, hot_in, moved_out, acc_out,
+    pos_ref, vel_ref, mass_ref, pair_ref, hot_ref,
     state, inverse, force, feature, push, target, weight_own, weight_far,
-    partial, sums, rho_rows, mid, send_sem, recv_sem,
+    partial, sums, rho_rows, mid, acc_ref, load_sem, send_sem, recv_sem,
 ):
     count_x, count_y, leaves, listed, slots = sizes
     extra = listed // base_entries - 1
@@ -57,13 +61,24 @@
     def device(a, b):
         return (jnp.clip(gx + a - 1, 0, count_x - 1), jnp.clip(gy + b - 1, 0, count_y - 1))
 
-    def sent(buffer, number, block):
+    rows4, half4 = 4 * leaves, 2 * leaves
+    messages = (
+        (state.at[0], 0, half4),
+        (state.at[0], half4, half4),
+        (state.at[1], 0, rows4),
+        (inverse, 0, leaves),
+        (force, 0, half4),
+        (force, half4, half4),
+    )
+
+    def sent(number, block):
+        buffer, first, count = messages[number]
         a, b = divmod(block, 3)
         to = (1, 2 - b) if a == 1 else (2 - a, 1)
         source = 4 if a == 1 or b == 1 else 3 + b
         descriptor = pltpu.make_async_remote_copy(
-            src_ref=buffer.at[source],
-            dst_ref=buffer.at[block],
+            src_ref=buffer.at[source, pl.ds(first, count)],
+            dst_ref=buffer.at[block, pl.ds(first, count)],
             send_sem=send_sem.at[number, block],
             recv_sem=recv_sem.at[number, block],
             device_id=device(*to),
@@ -71,16 +86,18 @@
         )
         return descriptor, inside(*to) if a == 1 or b == 1 else inside(2 - a, b)
 
-    def start(buffer, number, blocks):
+    def start(number, blocks):
         for block in blocks:
-            descriptor, valid = sent(buffer, number, block)
+            descriptor, valid = sent(number, block)
             pl.when(valid)(descriptor.start)
 
-    def arrive(buffer, number, blocks):
+    def arrive(number, blocks):
         for block in blocks:
-            pl.when(inside(*divmod(block, 3)))(sent(buffer, number, block)[0].wait_recv)
-
-    messages = (state.at[0], state.at[1], inverse, force)
+            pl.when(inside(*divmod(block, 3)))(sent(number, block)[0].wait_recv)
+
+    def relay(number):
+        arrive(number, (3, 5))
+        start(number, CORNERS)
 
     row = lax.broadcasted_iota(jnp.int32, (8, LEAF), 0)
     low = row < 4
@@ -95,6 +112,17 @@
         @pl.when(inside(a, b))
         def _():
             pl.semaphore_signal(barrier, inc=1, device_id=device(a, b), device_id_type=MESH)
+
+    loads = [
+        pltpu.make_async_copy(source, target_ref, load_sem.at[k])
+        for k, (source, target_ref) in enumerate(
+            ((pos_in, pos_ref), (vel_in, vel_ref), (mass_in, mass_ref), (pair_in, pair_ref), (hot_in, hot_ref))
+        )
+    ]
+    for load in loads:
+        load.start()
+    for load in loads:
+        load.wait()
 
     def lanes(component, pitch=4, count=leaves):
         return pl.ds(component, count, stride=pitch)
@@ -115,8 +143,8 @@
 
     own_state()
     pl.semaphore_wait(barrier, sum(inside(a, b).astype(jnp.int32) for a, b in sides_of))
-    for section in range(2):
-        start(messages[section], section, SIDES)
+    for number in range(3):
+        start(number, SIDES)
 
     for block in SIDES + CORNERS:
 
@@ -158,7 +186,7 @@
                         [halves[half], ones_rows], axis=0
                     ).astype(BF16)
 
-            loop(tiles, 8, one)
+            loop(tiles, tiles, one)
 
     def prepare_target(section):
         def one(i):
@@ -228,17 +256,17 @@
 
         def finish(index, value):
             if not first:
-                value = value + partial[index]
+                value = value + partial[section, index]
             if final:
                 rho_rows[pl.ds(index, 1), :] = jnp.sum(value.T, axis=0, keepdims=True)
             else:
-                partial[index] = value
+                partial[section, index] = value
 
         def base(i):
             ref = store_own.at[i, :, 0:LEAF] if first else store_far.at[i]
             finish(i, weigh(section, i, group, (0,), keep(ref, ...)))
 
-        loop(leaves, 16, base)
+        loop(leaves, leaves, base)
 
         def hot(s):
             leaf = slot_leaf(s)
@@ -258,7 +286,7 @@
                 )
             finish(leaves + s, value)
 
-        loop(slots, 4, hot)
+        loop(slots, slots, hot)
 
     def inverse_density():
         total = mass_ref[...] + rho_rows[pl.ds(0, leaves), :]
@@ -292,7 +320,7 @@
                     block, i, drive(shifted(here, block), velocity, spread(inverse, i, block))
                 )
 
-            loop(tiles, 4, one)
+            loop(tiles, tiles, one)
 
     def prepare_push2(blocks):
         for block in blocks:
@@ -309,7 +337,7 @@
                         )
                 store_push(block, i, tile)
 
-            loop(tiles, 4, one)
+            loop(tiles, tiles, one)
 
     def gather(section, leaf, blocks, offsets, weight):
         near = []
@@ -318,24 +346,31 @@
                 index = source(leaf, offset + block)
                 near.append(jnp.concatenate([feature[section, index], push[index]], axis=0))
         return lax.dot_general(
-            jnp.concatenate(near, axis=1), weight, (((1,), (1,)), ((), ())),
+            weight, jnp.concatenate(near, axis=1), (((1,), (1,)), ((), ())),
             preferred_element_type=F32,
-        )[0:CHANNELS]
-
-    def accumulate(section, group):
+        )
+
+    def accumulate(section, group, hot_too=True, chosen=None):
         first = group is OWN
+        final = group is CORNERS
         load_own = weight_own.at[section]
         load_far = weight_far.at[section, 0 if group is SIDES else 1]
 
         def finish(index, value):
-            rows = pl.ds(pl.multiple_of(CHANNELS * index, 8), CHANNELS)
-            sums[rows, :] = value if first else sums[rows, :] + value
+            kept = partial.at[section, index, :, 0:32]
+            if not first:
+                value = value + kept[...]
+            if final:
+                sums[pl.ds(CHANNELS * index, CHANNELS), :] = value.T[0:CHANNELS]
+            else:
+                kept[...] = value
 
         def base(i):
             weight = load_own[i, :, 0:LEAF] if first else load_far[i]
             finish(i, gather(section, i, group, (0,), weight))
 
-        loop(leaves, 16, base)
+        for i in range(leaves) if chosen is None else chosen:
+            base(i)
 
         def hot(s):
             leaf = slot_leaf(s)
@@ -355,25 +390,28 @@
                 )
             finish(leaves + s, value)
 
-        loop(slots, 4, hot)
-
-    def acceleration(section, q, velocity):
-        leaf = lax.broadcasted_iota(jnp.int32, (leaves, LEAF), 0)
+        if hot_too:
+            loop(slots, slots, hot)
+
+    def acceleration(section, first, count, q, velocity):
+        leaf = first + lax.broadcasted_iota(jnp.int32, (count, LEAF), 0)
         mine = [leaf == hot_ref[0, 0, s] for s in range(slots)]
 
         def channel(*rows):
-            both = functools.reduce(
-                jnp.add, [sums[lanes(r, CHANNELS, leaves + slots), :] for r in rows]
+            total = functools.reduce(
+                jnp.add, [sums[lanes(CHANNELS * first + r, CHANNELS, count), :] for r in rows]
             )
-            total = both[0:leaves]
+            hot = functools.reduce(
+                jnp.add, [sums[lanes(CHANNELS * leaves + r, CHANNELS, slots), :] for r in rows]
+            )
             for s in range(slots):
-                total = total + jnp.where(mine[s], both[leaves + s : leaves + s + 1], 0.0)
+                total = total + jnp.where(mine[s], hot[s : s + 1], 0.0)
             return total
 
         s1, sq = channel(8), channel(19, 23)
         result = []
         for d in range(3):
-            a = state[section, 4, lanes(d), :]
+            a = state[section, 4, lanes(4 * first + d, 4, count), :]
             result.append(
                 PUSH * (q * (a * s1 - channel(d, d + 4)) + a * sq)
                 + channel(16 + d, 20 + d)
@@ -384,70 +422,82 @@
     prepare_target(0)
     prepare(0, OWN)
     density(0, OWN)
-    arrive(messages[0], 0, (3, 5))
-    start(messages[0], 0, CORNERS)
     prepare_target(1)
-    arrive(messages[0], 0, (1, 7))
+    prepare(1, OWN)
+    density(1, OWN)
+    relay(0)
+    relay(1)
+
+    for number in (0, 1):
+        arrive(number, (1, 7))
     prepare(0, SIDES)
     density(0, SIDES)
-    arrive(messages[1], 1, (3, 5))
-    start(messages[1], 1, CORNERS)
-    prepare(1, OWN)
-    arrive(messages[0], 0, CORNERS)
+    for number in (0, 1):
+        arrive(number, CORNERS)
     prepare(0, CORNERS)
+    relay(2)
     density(0, CORNERS)
     inverse[4] = inverse_density()
-    start(inverse, 2, SIDES)
-
-    density(1, OWN)
-    arrive(messages[1], 1, (1, 7))
+    start(3, SIDES)
+
+    arrive(2, (1, 7))
     prepare(1, SIDES)
     density(1, SIDES)
-    arrive(inverse, 2, (3, 5))
-    start(inverse, 2, CORNERS)
-    arrive(messages[1], 1, CORNERS)
+    relay(3)
+    prepare_push1(OWN)
+    accumulate(0, OWN)
+    arrive(2, CORNERS)
     prepare(1, CORNERS)
     density(1, CORNERS)
     rho_rows[pl.ds(0, leaves), :] = inverse_density()
 
-    prepare_push1(OWN)
-    accumulate(0, OWN)
-    arrive(inverse, 2, (1, 7))
+    arrive(3, (1, 7))
     prepare_push1(SIDES)
     accumulate(0, SIDES)
-    arrive(inverse, 2, CORNERS)
+    arrive(3, CORNERS)
     prepare_push1(CORNERS)
-    accumulate(0, CORNERS)
-
-    velocity = [vel_ref[d] for d in range(3)]
-    acc = acceleration(0, inverse[4], velocity)
-    moved = [velocity[d] + 0.5 * time_step * acc[d] for d in range(3)]
-    q = rho_rows[pl.ds(0, leaves), :]
-    for d in range(3):
-        force[4, lanes(d), :] = q * (viscosity * moved[d] - PUSH * state[1, 4, lanes(d), :])
-        mid[d] = moved[d]
-        disp_ref[d] = time_step * moved[d]
-    force[4, lanes(3), :] = q
-    start(force, 3, SIDES)
+    half = leaves // 2
+    for part in range(2):
+        first = part * half
+        accumulate(0, CORNERS, part == 0, range(first, first + half))
+        here = pl.ds(first, half)
+        velocity = [vel_ref[d, here, :] for d in range(3)]
+        acc = acceleration(0, first, half, inverse[4, here, :], velocity)
+        q = rho_rows[here, :]
+        for d in range(3):
+            moved = velocity[d] + 0.5 * time_step * acc[d]
+            mid[d, here, :] = moved
+            rows = lanes(4 * first + d, 4, half)
+            force[4, rows, :] = q * (viscosity * moved - PUSH * state[1, 4, rows, :])
+        force[4, lanes(4 * first + 3, 4, half), :] = q
+        start(4 + part, SIDES)
+    stores = [pltpu.make_async_copy(mid, moved_out, load_sem.at[0])]
+    stores[0].start()
+
     prepare_push2(OWN)
     accumulate(1, OWN)
-    arrive(force, 3, (3, 5))
-    start(force, 3, CORNERS)
-    arrive(force, 3, (1, 7))
+    relay(4)
+    relay(5)
+    for number in (4, 5):
+        arrive(number, (1, 7))
     prepare_push2(SIDES)
     accumulate(1, SIDES)
-    arrive(force, 3, CORNERS)
+    for number in (4, 5):
+        arrive(number, CORNERS)
     prepare_push2(CORNERS)
     accumulate(1, CORNERS)
-
-    acc = acceleration(1, rho_rows[pl.ds(0, leaves), :], [mid[d] for d in range(3)])
+    acc = acceleration(1, 0, leaves, rho_rows[pl.ds(0, leaves), :], [mid[d] for d in range(3)])
     for d in range(3):
-        newv_ref[d] = vel_ref[d] + time_step * acc[d]
-
-    for number, buffer in enumerate(messages):
+        acc_ref[d] = acc[d]
+    stores.append(pltpu.make_async_copy(acc_ref, acc_out, load_sem.at[1]))
+    stores[1].start()
+
+    for number in range(len(messages)):
         for block in SIDES + CORNERS:
-            descriptor, valid = sent(buffer, number, block)
+            descriptor, valid = sent(number, block)
             pl.when(valid)(descriptor.wait_send)
+    for store in stores:
+        store.wait()
 
 
 def local(position, velocity, mass, pair_list, hot_leaf):
@@ -455,15 +505,19 @@
     slots = hot_leaf.shape[2]
     extra = listed // base_entries - 1
     sizes = (lax.axis_size("gx"), lax.axis_size("gy"), leaves, listed, slots)
-    vmem = pl.BlockSpec(memory_space=pltpu.VMEM)
-    smem = pl.BlockSpec(memory_space=pltpu.SMEM)
+    anywhere = pl.BlockSpec(memory_space=pl.ANY)
     shape = jax.ShapeDtypeStruct((3, leaves, LEAF), F32)
-    outs = pl.pallas_call(
+    moved, acc = pl.pallas_call(
         functools.partial(kernel, sizes),
         out_shape=[shape, shape],
-        in_specs=[vmem] * 3 + [smem] * 2,
-        out_specs=[vmem] * 2,
+        in_specs=[anywhere] * 5,
+        out_specs=[anywhere] * 2,
         scratch_shapes=[
+            pltpu.VMEM((3, leaves, LEAF), F32),
+            pltpu.VMEM((3, leaves, LEAF), F32),
+            pltpu.VMEM((leaves, LEAF), F32),
+            pltpu.SMEM((1, listed, 1, leaves), jnp.int32),
+            pltpu.SMEM((1, 1, slots), jnp.int32),
             pltpu.VMEM((2, 9, 4 * leaves, LEAF), F32),
             pltpu.VMEM((9, leaves, LEAF), F32),
             pltpu.VMEM((9, 4 * leaves, LEAF), F32),
@@ -472,12 +526,14 @@
             pltpu.VMEM((2, leaves, LEAF, LEAF), BF16),
             pltpu.VMEM((2, leaves + slots, LEAF, extra * LEAF), BF16),
             pltpu.VMEM((2, 2, leaves + extra * slots, LEAF, 4 * LEAF), BF16),
-            pltpu.VMEM((leaves + slots, LEAF, LEAF), F32),
+            pltpu.VMEM((2, leaves + slots, LEAF, LEAF), F32),
             pltpu.VMEM(((leaves + slots) * CHANNELS, LEAF), F32),
             pltpu.VMEM((leaves + slots, LEAF), F32),
             pltpu.VMEM((3, leaves, LEAF), F32),
-            pltpu.SemaphoreType.DMA((4, 9)),
-            pltpu.SemaphoreType.DMA((4, 9)),
+            pltpu.VMEM((3, leaves, LEAF), F32),
+            pltpu.SemaphoreType.DMA((5,)),
+            pltpu.SemaphoreType.DMA((6, 9)),
+            pltpu.SemaphoreType.DMA((6, 9)),
         ],
         compiler_params=pltpu.CompilerParams(
             collective_id=0, has_side_effects=True, vmem_limit_bytes=60 * 2**20
@@ -489,7 +545,10 @@
         jnp.transpose(pair_list, (0, 3, 1, 2)),
         hot_leaf,
     )
-    return tuple(out.reshape(position.shape) for out in outs)
+    return (
+        (time_step * moved).reshape(position.shape),
+        (velocity.reshape(3, leaves, LEAF) + time_step * acc).reshape(position.shape),
+    )
 
 
 def solution(mesh):

time: 44.6 us -> 36.8 us (0.83)
  Pallas kernels: 41.7 us -> 34.3 us
  local copies, waits for them, and re-layouts: 2.06 us -> 0.01 us
  other arithmetic: 0 us -> 1.47 us
    pallas_call x1, Pallas kernels: 41.7 us -> 34.3 us  [local(): pl.pallas_call(functools.partial(kernel, sizes), out_shape=[shape, shape]...]
    unnamed x4 -> x2, local copies, waits for them, and re-layouts: 2.06 us -> 0.01 us
    add x0 -> x1, other arithmetic: none -> 1.47 us  [local(): velocity.reshape(3, leaves, LEAF) + time_step * acc]
where the time goes in v3:
time: 36.8 us; the launch traced here: 36.4 us
  Pallas kernels  34.3 us (93%)
  other arithmetic  1.47 us (4%)
  between operations  0.66 us (2%)
    pallas_call x1, Pallas kernels, local(): pl.pallas_call(functools.partial(kernel, sizes), out_shape=[shape, shape]...  34.3 us
    add x1, other arithmetic, local(): velocity.reshape(3, leaves, LEAF) + time_step * acc  1.47 us

profile of v3, /device:TPU:17, one launch (start us, length us, event | category | flops | bytes accessed | tf_op | source)
XLA Modules:
  0.0 36.4 jit_solution(11840231476733295983)
XLA Ops:
  0.6 0.0 copy-start
  0.6 34.3 %shard_map.68 = (f32[3,32,128]{2,1,0:T(8,128)}, f32[3,32,128]{2,1,0:T(8,128)}) custom-call(f32[3,32,128]{2,1,0:T(8,128)} %bitcast.8, f32[3,32,128]{2,1,0:T(8,128)} %bitcast.6, f32[32,128]{1,0:T(8,128)} %bitcast.11, s32[1,27,1,32]{3,2,1,0:T(1,128)} %bitcast.12, s32[1,1,8]{2,1,0:T(1,128)} %hot_in.1), custom_call_target="tpu_custom_call" | custom-call | tf_op jit(solution)/shard_map/pallas_call | solution.py:510
  34.9 0.0 copy-done
  34.9 1.5 %multiply_add_fusion = (f32[3,32,128]{2,1,0:T(8,128)}, f32[3,32,128]{2,1,0:T(8,128)}) fusion(f32[3,32,128]{2,1,0:T(8,128)S(1)} %bitcast.7, f32[3,32,128]{2,1,0:T(8,128)} %get-tuple-element.5, f32[3,32,128]{2,1,0:T(8,128)} %get-tuple-element.4), kind=kLoop, calls=%fused_computation | loop fusion | flops 36864 | bytes 245760 | tf_op jit(solution)/shard_map/add | solution.py:550
Async XLA Ops:
  0.6 34.3 %copy-start = (f32[1,1,3,4096]{3,1,2,0:T(1,128)S(1)}, f32[1,1,3,4096]{3,1,2,0:T(1,128)}, u32[]{:S(2)}) copy-start(f32[1,1,3,4096]{3,1,2,0:T(1,128)} %param.6) | copy-start | bytes 147460

commit v4 on v3

--- a/solution.py
+++ b/solution.py
@@ -443,11 +443,11 @@
     arrive(2, (1, 7))
     prepare(1, SIDES)
     density(1, SIDES)
-    relay(3)
     prepare_push1(OWN)
     accumulate(0, OWN)
     arrive(2, CORNERS)
     prepare(1, CORNERS)
+    relay(3)
     density(1, CORNERS)
     rho_rows[pl.ds(0, leaves), :] = inverse_density()
 

time: 36.8 us -> 36.1 us (0.981)
  Pallas kernels: 34.3 us -> 33.5 us
    pallas_call x1, Pallas kernels: 34.3 us -> 33.5 us  [local(): pl.pallas_call(functools.partial(kernel, sizes), out_shape=[shape, shape]...]
where the time goes in v4:
time: 36.1 us; the launch traced here: 35.6 us
  Pallas kernels  33.5 us (93%)
  other arithmetic  1.47 us (4%)
  between operations  0.66 us (2%)
    pallas_call x1, Pallas kernels, local(): pl.pallas_call(functools.partial(kernel, sizes), out_shape=[shape, shape]...  33.5 us
    add x1, other arithmetic, local(): velocity.reshape(3, leaves, LEAF) + time_step * acc  1.47 us

profile of v4, /device:TPU:17, one launch (start us, length us, event | category | flops | bytes accessed | tf_op | source)
XLA Modules:
  0.0 35.6 jit_solution(15152000794401545662)
XLA Ops:
  0.6 0.0 copy-start
  0.6 33.5 %shard_map.68 = (f32[3,32,128]{2,1,0:T(8,128)}, f32[3,32,128]{2,1,0:T(8,128)}) custom-call(f32[3,32,128]{2,1,0:T(8,128)} %bitcast.8, f32[3,32,128]{2,1,0:T(8,128)} %bitcast.6, f32[32,128]{1,0:T(8,128)} %bitcast.11, s32[1,27,1,32]{3,2,1,0:T(1,128)} %bitcast.12, s32[1,1,8]{2,1,0:T(1,128)} %hot_in.1), custom_call_target="tpu_custom_call" | custom-call | tf_op jit(solution)/shard_map/pallas_call | solution.py:510
  34.1 0.0 copy-done
  34.1 1.5 %multiply_add_fusion = (f32[3,32,128]{2,1,0:T(8,128)}, f32[3,32,128]{2,1,0:T(8,128)}) fusion(f32[3,32,128]{2,1,0:T(8,128)S(1)} %bitcast.7, f32[3,32,128]{2,1,0:T(8,128)} %get-tuple-element.5, f32[3,32,128]{2,1,0:T(8,128)} %get-tuple-element.4), kind=kLoop, calls=%fused_computation | loop fusion | flops 36864 | bytes 245760 | tf_op jit(solution)/shard_map/add | solution.py:550
Async XLA Ops:
  0.6 33.5 %copy-start = (f32[1,1,3,4096]{3,1,2,0:T(1,128)S(1)}, f32[1,1,3,4096]{3,1,2,0:T(1,128)}, u32[]{:S(2)}) copy-start(f32[1,1,3,4096]{3,1,2,0:T(1,128)} %param.6) | copy-start | bytes 147460
